TPU v7x, 32 devices: a whole 2x2x4 slice. The times are simulated.
32 devices in a mesh: band: 8 (over z, x), grid: 4 (over y, core).
Axes of the slice: x: 2, y: 2, z: 4, core: 2. Of those that a mesh axis runs over, the one named last changes fastest.
Arguments:
- partial_density: float32 [8, 128, 128, 128], P('band', 'grid'), may hold values from 0.01 to 1
- node_index: int32 [128, 128, 128], P('grid'), may hold values from 0 to 19
- node_weight: float32 [4, 128, 128, 128], P(None, 'grid'), may hold values from 0 to 1
- node_slope: float32 [4, 128, 128, 128], P(None, 'grid'), may hold values from -6 to 6
- kernel_table: float32 [20, 20, 114], replicated, may hold values from -0.8 to 0.8, as said below
Outputs:
- potential: float32 [128, 128, 128], P('grid')
Inputs may be any that keep to these rules, and one draw needn't show every extreme that they name: node_index(r) is the node at the lower end of the interval of q0 at r; nodes node_index - 1 to node_index + 2 carry the four weights. `kernel_table`: symmetric in its first two indices.
All inputs are finite; a program needn't handle non-finite values.
Results may differ from a plain program's by a relative error of at most 0.0003.
Values sent between devices are 32-bit elements; how exact they have to be, the bound alone decides.
A program may use at most 128 MiB of HBM per device.

v0:
```python
import math
import jax
import jax.numpy as jnp
from jax import lax
from jax.sharding import PartitionSpec as P

N = 128


def frequency_of(positions, length):
    return jnp.where(positions < length // 2, positions, positions - length)


def shell_split(square_norm):
    root_value = jnp.sqrt(square_norm.astype(jnp.float32))
    shell_idx = root_value.astype(jnp.int32)
    shell_idx = shell_idx - (shell_idx * shell_idx > square_norm).astype(jnp.int32)
    shell_idx = shell_idx + ((shell_idx + 1) * (shell_idx + 1) <= square_norm).astype(jnp.int32)
    fraction = root_value - shell_idx.astype(jnp.float32)
    return (shell_idx, fraction)


def node_fields(count_nodes, intervals, weights):
    node_ids = jnp.arange(count_nodes, dtype=jnp.int32)
    summed = jnp.zeros((count_nodes,) + intervals.shape, jnp.float32)
    for offset in range(4):
        matched = node_ids[:, None, None, None] == (intervals + (offset - 1))[None]
        summed = summed + jnp.where(matched, weights[offset][None], jnp.zeros((), jnp.float32))
    return summed


def phase_table(source_idx, target_idx, modulus):
    product_mod = source_idx[:, None] * target_idx[None, :] % modulus
    angles = product_mod.astype(jnp.float32) * (2.0 * math.pi / modulus)
    return (jnp.cos(angles), jnp.sin(angles))


def contract(pattern, operand, matrix):
    return jnp.einsum(pattern, operand, matrix, precision=lax.Precision.HIGHEST)


def mirrored(values, dim):
    return jnp.roll(jnp.flip(values, dim), 1, dim)


def forward_tables(positions, plane_ids, length):
    cosine, sine = phase_table(positions, plane_ids, length)
    alternating = jnp.where(positions % 2 == 0, 1.0, -1.0).astype(jnp.float32)
    sine = jnp.where(plane_ids[None, :] == 0, -alternating[:, None], sine)
    return (cosine, sine)


def shell_weights_of(square_norm, shell_count):
    shell_ids = jnp.arange(shell_count, dtype=jnp.int32)
    shell_idx, fraction = shell_split(square_norm)
    expand = (slice(None),) + (None,) * square_norm.ndim
    lower_hit = shell_ids[expand] == shell_idx[None]
    upper_hit = shell_ids[expand] == shell_idx[None] + 1
    return jnp.where(lower_hit, 1.0 - fraction[None], 0.0) + jnp.where(
        upper_hit, fraction[None], 0.0
    )


def per_device(partial_density, node_index, node_weight, node_slope, kernel_table):
    length = N
    half = length // 2
    count_nodes = kernel_table.shape[0]
    shell_count = kernel_table.shape[2]
    planes = half // lax.axis_size("band")
    grid_part = length // lax.axis_size("grid")
    band_at = lax.axis_index("band")
    grid_at = lax.axis_index("grid")
    full_range = jnp.arange(length, dtype=jnp.int32)
    own_planes = band_at * planes + jnp.arange(planes, dtype=jnp.int32)
    own_rows = grid_at * grid_part + jnp.arange(grid_part, dtype=jnp.int32)
    first_band = band_at == 0
    lower_rows = (full_range >= 1) & (full_range < half)
    upper_rows = full_range > half
    density = lax.psum(partial_density[0], "band")
    theta_fields = density[None] * node_fields(count_nodes, node_index, node_weight)
    cosine_z, sine_z = forward_tables(full_range, own_planes, length)
    forward_real = contract("axyz,zk->axyk", theta_fields, cosine_z)
    forward_imag = -contract("axyz,zk->axyk", theta_fields, sine_z)
    columns = jnp.stack([forward_real, forward_imag])
    cosine_full, sine_full = phase_table(full_range, full_range, length)
    y_cos = contract("caxyp,yw->caxpw", columns, cosine_full)
    y_sin = contract("caxyp,yw->caxpw", columns, sine_full)
    ywave_real = y_cos[0] + y_sin[1]
    ywave_imag = y_cos[1] - y_sin[0]
    first_real = ywave_real[:, :, 0, :]
    first_imag = ywave_imag[:, :, 0, :]
    turned_real = mirrored(first_real, 2)
    turned_imag = mirrored(first_imag, 2)
    packed_real = jnp.where(
        lower_rows,
        0.5 * (first_real + turned_real),
        jnp.where(upper_rows, 0.5 * (turned_imag + first_imag), first_real),
    )
    packed_imag = jnp.where(
        lower_rows,
        0.5 * (first_imag - turned_imag),
        jnp.where(upper_rows, 0.5 * (first_real - turned_real), first_imag),
    )
    ywave_real = ywave_real.at[:, :, 0, :].set(jnp.where(first_band, packed_real, first_real))
    ywave_imag = ywave_imag.at[:, :, 0, :].set(jnp.where(first_band, packed_imag, first_imag))
    pencils = lax.all_to_all(
        jnp.stack([ywave_real, ywave_imag]), "grid", split_axis=4, concat_axis=2, tiled=True
    )
    x_cos = contract("caxpw,xv->capwv", pencils, cosine_full)
    x_sin = contract("caxpw,xv->capwv", pencils, sine_full)
    spec_real = x_cos[0] + x_sin[1]
    spec_imag = x_cos[1] - x_sin[0]
    freq_x = frequency_of(full_range, length)
    square_x = freq_x * freq_x
    freq_rows = frequency_of(own_rows, length)
    plane_square = own_planes * own_planes
    third_square = jnp.where(
        (own_planes[:, None] == 0) & (own_rows[None, :] > half), half * half, plane_square[:, None]
    )
    special_rows = ((own_rows == 0) | (own_rows == half)) & (own_planes[0] == 0)

    def mix_row(row_idx):
        row_real = lax.dynamic_index_in_dim(spec_real, row_idx, 2, keepdims=False)
        row_imag = lax.dynamic_index_in_dim(spec_imag, row_idx, 2, keepdims=False)
        freq_row = lax.dynamic_index_in_dim(freq_rows, row_idx, 0, keepdims=False)
        third_row = lax.dynamic_index_in_dim(third_square, row_idx, 1, keepdims=False)
        square_norm = third_row[:, None] + square_x[None, :] + freq_row * freq_row
        kernel = contract("abs,spx->abpx", kernel_table, shell_weights_of(square_norm, shell_count))
        out_real = contract("abpx,apx->bpx", kernel, row_real)
        out_imag = contract("abpx,apx->bpx", kernel, row_imag)
        other_norm = square_x + freq_row * freq_row + half * half
        kernel_other = contract(
            "abs,sx->abx", kernel_table, shell_weights_of(other_norm, shell_count)
        )
        flag = lax.dynamic_index_in_dim(special_rows, row_idx, 0, keepdims=False).astype(
            jnp.float32
        )
        spread = 0.5 * flag * (kernel[:, :, 0, :] - kernel_other)
        base_real = row_real[:, 0, :]
        base_imag = row_imag[:, 0, :]
        delta_real = mirrored(base_real, 1) - base_real
        delta_imag = -mirrored(base_imag, 1) - base_imag
        out_real = out_real.at[:, 0, :].add(contract("abx,ax->bx", spread, delta_real))
        out_imag = out_imag.at[:, 0, :].add(contract("abx,ax->bx", spread, delta_imag))
        return jnp.stack([out_real, out_imag])

    mixed = lax.map(mix_row, jnp.arange(grid_part, dtype=jnp.int32))
    i_cos = contract("wcbpx,xv->wcbpv", mixed, cosine_full)
    i_sin = contract("wcbpx,xv->wcbpv", mixed, sine_full)
    inverse_real = i_cos[:, 0] - i_sin[:, 1]
    inverse_imag = i_cos[:, 1] + i_sin[:, 0]
    returned = lax.all_to_all(
        jnp.stack([inverse_real, inverse_imag], axis=1),
        "grid",
        split_axis=4,
        concat_axis=0,
        tiled=True,
    )
    lower_col = lower_rows[:, None, None]
    upper_col = upper_rows[:, None, None]
    back_real = returned[:, 0, :, 0, :]
    back_imag = returned[:, 1, :, 0, :]
    flip_real = mirrored(back_real, 0)
    flip_imag = mirrored(back_imag, 0)
    joined_real = jnp.where(
        lower_col, back_real - flip_imag, jnp.where(upper_col, flip_real + back_imag, back_real)
    )
    joined_imag = jnp.where(
        lower_col, back_imag + flip_real, jnp.where(upper_col, back_real - flip_imag, back_imag)
    )
    returned = returned.at[:, 0, :, 0, :].set(jnp.where(first_band, joined_real, back_real))
    returned = returned.at[:, 1, :, 0, :].set(jnp.where(first_band, joined_imag, back_imag))
    b_cos = contract("wcbpx,wy->cbpxy", returned, cosine_full)
    b_sin = contract("wcbpx,wy->cbpxy", returned, sine_full)
    slab_real = b_cos[0] - b_sin[1]
    slab_imag = b_cos[1] + b_sin[0]
    cosine_own, sine_own = phase_table(own_planes, full_range, length)
    alternating = jnp.where(full_range % 2 == 0, 1.0, -1.0).astype(jnp.float32)
    cosine_back = jnp.where(own_planes[:, None] == 0, 1.0, 2.0 * cosine_own)
    sine_back = jnp.where(own_planes[:, None] == 0, -alternating[None, :], 2.0 * sine_own)
    scale_factor = 1.0 / float(length) ** 3
    field_parts = (
        contract("bpxy,pz->bxyz", slab_real, cosine_back)
        - contract("bpxy,pz->bxyz", slab_imag, sine_back)
    ) * scale_factor
    slopes = node_fields(count_nodes, node_index, node_slope)
    partial_potential = jnp.sum(field_parts * slopes, axis=0)
    return lax.psum(partial_potential, "band")


def solution(mesh):
    placed = (
        P("band", "grid", None, None),
        P("grid", None, None),
        P(None, "grid", None, None),
        P(None, "grid", None, None),
        P(),
    )
    return jax.shard_map(
        per_device, mesh=mesh, in_specs=placed, out_specs=P("grid", None, None), check_vma=False
    )
```

profile of v0, /device:TPU:0, one launch (start us, length us, event | category | flops | bytes accessed | tf_op | source)
XLA Modules:
  0.0 1415.7 jit_solution(10311914120012794032)
XLA Ops:
  17.1 98.9 %all-reduce.3.cloned.1.call-done = f32[32,128,128]{2,1,0:T(8,128)} async-done(((f32[32,128,128]{2,1,0:T(8,128)}), f32[32,128,128]{2,1,0:T(8,128)}) %all-reduce.3.cloned.1.call-update) | async-done | bytes 2097168 | tf_op jit(solution)/shard_map/psum | solution.py:79
  116.0 66.0 %fusion.70 = f32[1,20,32,128,8]{3,4,2,1,0:T(8,128)} fusion(f32[32,128,128]{2,1,0:T(8,128)} %get-tuple-element.295, s32[32,128,128]{2,1,0:T(8,128)} %get-tuple-element.309, f32[32,128,128]{2,1,0:T(8,128)} %get-tuple-element.296, s32[32,128,128]{2,1,0:T(8,128)} %get-tuple-element.310, f32[32,128,128]{2,1,0:T(8,128)} %get-tuple-element.294, ...), kind=kOutput, calls=%fused_computation.132 | convolution fusion | flops 1132476416 | bytes 21495840 | tf_op jit(solution)/shard_map/axyz,zk->axyk/dot_general | solution.py:39
  182.0 57.5 %negate_bitcast_fusion = f32[1,20,32,128,8]{3,4,2,1,0:T(8,128)} fusion(f32[32,128,128]{2,1,0:T(8,128)} %get-tuple-element.295, s32[32,128,128]{2,1,0:T(8,128)} %get-tuple-element.309, f32[32,128,128]{2,1,0:T(8,128)} %get-tuple-element.296, s32[32,128,128]{2,1,0:T(8,128)} %get-tuple-element.310, f32[32,128,128]{2,1,0:T(8,128)} %get-tuple-element.294, ...), kind=kOutput, calls=%fused_computation.123 | convolution fusion | flops 1133132800 | bytes 21496360 | tf_op jit(solution)/shard_map/axyz,zk->axyk/dot_general | solution.py:39
  266.0 7.4 scatter.15
  273.4 9.3 scatter.14
  287.3 17.6 %copy.61 = f32[2,20,32,8,128]{2,3,1,0,4:T(8,128)} copy(f32[2,20,32,8,128]{4,3,2,1,0:T(8,128)} %pad_maximum_fusion.1) | data formatting | bytes 10485760 | tf_op jit(solution)/shard_map/stack | solution.py:107
  304.9 23.5 %reshape.667 = f32[4,1,327680]{2,1,0:T(1,128)} reshape(f32[128,2,20,8,32]{4,3,2,1,0:T(8,128)} %bitcast.306) | data formatting | bytes 10485760
  333.6 59.3 %all-to-all-done = f32[4,1,327680]{2,1,0:T(1,128)} async-done(((f32[4,1,327680]{2,1,0:T(1,128)}), f32[4,1,327680]{2,1,0:T(1,128)}, u32[]{:S(2)}, u32[]{:S(2)}) %all-to-all-start) | async-done | bytes 5242912 | tf_op jit(solution)/shard_map/all_to_all | solution.py:106
  393.5 17.9 %reduce.21 = f32[4,327680]{1,0:T(4,128)} reduce(f32[4,1,327680]{2,1,0:T(1,128)} %all-to-all-done, f32[]{:T(128)} %broadcast.766), dimensions={1}, to_apply=%all_to_all.26.reduce_sub_computation | reduce | bytes 10485764 | tf_op jit(solution)/shard_map/all_to_all | solution.py:106
  411.4 16.7 %reshape.668 = f32[128,2,20,8,32]{4,3,2,1,0:T(8,128)} reshape(f32[4,327680]{1,0:T(4,128)} %reduce.21) | data formatting | bytes 10485760
  428.1 25.8 %copy.142 = f32[2,20,32,8,4,32]{2,4,5,3,1,0:T(4,128)} copy(f32[2,20,32,8,4,32]{2,3,1,0,5,4:T(8,128)} %bitcast.307) | data formatting | bytes 10485760 | tf_op jit(solution)/shard_map/all_to_all | solution.py:106
  453.9 16.5 %all_to_all.29 = f32[2,20,128,8,32]{2,4,3,1,0:T(8,128)} reshape(f32[2,20,4,32,8,32]{3,2,5,4,1,0:T(4,128)} %bitcast.308) | data formatting | bytes 10485760 | tf_op jit(solution)/shard_map/all_to_all | solution.py:106
  470.4 8.7 fusion.81
  486.7 425.2 %while.20 = (s32[]{:T(128)}, f32[32,2,20,8,128]{4,3,2,1,0:T(8,128)}, s32[32]{0:T(128)S(1)}, f32[20,8,32,128]{3,2,1,0:T(8,128)}, s32[8,32]{0,1:T(8,128)S(1)}, /*i...) while((s32[]{:T(128)}, ...), condition=%wide.region_2.3_spmd.clone.clone, body=%wide.region_1.2_spmd.clone.clone.sunk | while | flops 633025536 | bytes 4581378 | solution.py:147
  927.4 17.5 %copy.63 = f32[32,2,20,8,128]{0,3,2,1,4:T(8,128)} copy(f32[32,2,20,8,128]{4,3,2,1,0:T(8,128)} %pad_maximum_fusion.2) | data formatting | bytes 10485760 | tf_op jit(solution)/shard_map/stack | solution.py:153
  945.0 23.5 %reshape.669 = f32[4,1,327680]{2,1,0:T(1,128)} reshape(f32[128,2,20,8,32]{4,3,2,1,0:T(8,128)} %bitcast.309) | data formatting | bytes 10485760
  979.9 53.0 %all-to-all-done.1 = f32[4,1,327680]{2,1,0:T(1,128)} async-done(((f32[4,1,327680]{2,1,0:T(1,128)}), f32[4,1,327680]{2,1,0:T(1,128)}, u32[]{:S(2)}, u32[]{:S(2)}) %all-to-all-start.1) | async-done | bytes 5242912 | tf_op jit(solution)/shard_map/all_to_all | solution.py:152
  1033.0 18.3 %reduce.22 = f32[4,327680]{1,0:T(4,128)} reduce(f32[4,1,327680]{2,1,0:T(1,128)} %all-to-all-done.1, f32[]{:T(128)} %broadcast.766), dimensions={1}, to_apply=%all_to_all.30.reduce_sub_computation | reduce | bytes 10485764 | tf_op jit(solution)/shard_map/all_to_all | solution.py:152
  1051.3 16.7 %reshape.670 = f32[128,2,20,8,32]{4,3,2,1,0:T(8,128)} reshape(f32[4,327680]{1,0:T(4,128)} %reduce.22) | data formatting | bytes 10485760
  1068.0 25.5 %copy.64 = f32[4,32,2,20,8,32]{1,0,5,3,4,2:T(4,128)} copy(f32[4,32,2,20,8,32]{1,4,3,2,5,0:T(8,128)} %bitcast.310) | data formatting | bytes 10485760 | tf_op jit(solution)/shard_map/all_to_all | solution.py:152
  1093.5 16.6 %all_to_all.33 = f32[128,2,20,8,32]{0,4,2,3,1:T(8,128)} reshape(f32[4,32,2,20,8,32]{1,0,5,3,4,2:T(4,128)} %copy.64) | data formatting | bytes 10485760 | tf_op jit(solution)/shard_map/all_to_all | solution.py:152
  1138.9 69.8 %fusion.68 = f32[20,32,128,128]{3,2,1,0:T(8,128)} fusion(f32[20,8,32,128]{3,2,1,0:T(8,128)S(1)} %get-tuple-element.284, s32[8]{0:T(128)S(1)} %iota_add_fusion.1, pred[8]{0:T(512)(128)(4,1)S(1)} %broadcast_compare_fusion), kind=kOutput, calls=%fused_computation.121 | convolution fusion | flops 1006649344 | bytes 44564520 | tf_op jit(solution)/shard_map/bpxy,pz->bxyz/dot_general | solution.py:39
  1208.8 95.9 %multiply_reduce_fusion.4 = f32[32,128,128]{2,1,0:T(8,128)} fusion(f32[20,32,128,128]{3,2,1,0:T(8,128)} %fusion.68, f32[32,128,128]{2,1,0:T(8,128)S(1)} %copy-done.6, f32[32,128,128]{2,1,0:T(8,128)S(1)} %copy-done.7, f32[32,128,128]{2,1,0:T(8,128)S(1)} %copy-done.5, f32[32,128,128]{2,1,0:T(8,128)S(1)} %get-tuple-element.289, ...), kind=kOutput, calls=%fused_computation.74 | convolution fusion | flops 1163411456 | bytes 63439400 | tf_op jit(solution)/shard_map/bpxy,pz->bxyz/dot_general | solution.py:39
  1304.7 100.9 %all-reduce.5.cloned.1.call-done = f32[32,128,128]{2,1,0:T(8,128)} async-done(((f32[32,128,128]{2,1,0:T(8,128)}), f32[32,128,128]{2,1,0:T(8,128)}) %all-reduce.5.cloned.1.call-update) | async-done | bytes 2097168 | tf_op jit(solution)/shard_map/psum | solution.py:188
  (1141 shorter events, 410.1 us)
Async XLA Ops:
  6.5 109.5 %all-reduce.3.cloned.1.call-start = ((), (), s32[]{:S(2)}) async-start(), calls=%async_computation.2 | async-start | bytes 4194304 | tf_op jit(solution)/shard_map/psum | solution.py:79
  7.3 6.2 copy-start.12
  7.3 174.7 %copy-start.14 = (f32[128]{0:T(128)}, f32[128]{0:T(128)S(1)}, u32[]{:S(2)}) copy-start(f32[128]{0:T(128)S(1)} %fusion.141) | copy-start | bytes 1540
  13.5 102.5 %copy-start = (s32[32,128,128]{2,1,0:T(8,128)S(1)}, s32[32,128,128]{2,1,0:T(8,128)}, u32[]{:S(2)}) copy-start(s32[32,128,128]{2,1,0:T(8,128)} %param.20) | copy-start | bytes 6291460
  239.5 7.3 copy-start.10
  239.5 7.3 copy-start.11
  328.4 64.5 %all-to-all-start = ((f32[4,1,327680]{2,1,0:T(1,128)}), f32[4,1,327680]{2,1,0:T(1,128)}, u32[]{:S(2)}, u32[]{:S(2)}) async-start(f32[4,1,327680]{2,1,0:T(1,128)} %reshape.667), calls=%async_computation | async-start | bytes 10485760 | tf_op jit(solution)/shard_map/all_to_all | solution.py:106
  470.4 8.8 copy-start.8
  483.6 3.1 copy-start.13
  911.9 7.2 copy-start.9
  968.5 64.5 %all-to-all-start.1 = ((f32[4,1,327680]{2,1,0:T(1,128)}), f32[4,1,327680]{2,1,0:T(1,128)}, u32[]{:S(2)}, u32[]{:S(2)}) async-start(f32[4,1,327680]{2,1,0:T(1,128)} %reshape.669), calls=%async_computation.1 | async-start | bytes 10485760 | tf_op jit(solution)/shard_map/all_to_all | solution.py:152
  973.5 432.0 %all-reduce.5.cloned.1.call-start = ((), (), s32[]{:S(2)}) async-start(), calls=%async_computation.3 | async-start | bytes 4194304 | tf_op jit(solution)/shard_map/psum | solution.py:188
  1138.8 69.9 %copy-start.1 = (s32[32,128,128]{2,1,0:T(8,128)S(1)}, s32[32,128,128]{2,1,0:T(8,128)}, u32[]{:S(2)}) copy-start(s32[32,128,128]{2,1,0:T(8,128)} %param.20) | copy-start | bytes 6291460
  1138.8 69.9 %copy-start.2 = (s32[32,128,128]{2,1,0:T(8,128)S(1)}, s32[32,128,128]{2,1,0:T(8,128)}, u32[]{:S(2)}) copy-start(s32[32,128,128]{2,1,0:T(8,128)} %get-tuple-element.308) | copy-start | bytes 6291460
  1138.8 69.9 %copy-start.3 = (s32[32,128,128]{2,1,0:T(8,128)S(1)}, s32[32,128,128]{2,1,0:T(8,128)}, u32[]{:S(2)}) copy-start(s32[32,128,128]{2,1,0:T(8,128)} %get-tuple-element.309) | copy-start | bytes 6291460
  1138.8 69.9 %copy-start.4 = (s32[32,128,128]{2,1,0:T(8,128)S(1)}, s32[32,128,128]{2,1,0:T(8,128)}, u32[]{:S(2)}) copy-start(s32[32,128,128]{2,1,0:T(8,128)} %get-tuple-element.310) | copy-start | bytes 6291460
  1138.8 69.9 %copy-start.5 = (f32[32,128,128]{2,1,0:T(8,128)S(1)}, f32[32,128,128]{2,1,0:T(8,128)}, u32[]{:S(2)}) copy-start(f32[32,128,128]{2,1,0:T(8,128)} %get-tuple-element.290) | copy-start | bytes 6291460
  1138.8 69.9 %copy-start.6 = (f32[32,128,128]{2,1,0:T(8,128)S(1)}, f32[32,128,128]{2,1,0:T(8,128)}, u32[]{:S(2)}) copy-start(f32[32,128,128]{2,1,0:T(8,128)} %get-tuple-element.291) | copy-start | bytes 6291460
  1138.8 69.9 %copy-start.7 = (f32[32,128,128]{2,1,0:T(8,128)S(1)}, f32[32,128,128]{2,1,0:T(8,128)}, u32[]{:S(2)}) copy-start(f32[32,128,128]{2,1,0:T(8,128)} %get-tuple-element.292) | copy-start | bytes 6291460
  1138.8 69.9 %copy-start.15 = (f32[128]{0:T(128)S(1)}, f32[128]{0:T(128)}, u32[]{:S(2)}) copy-start(f32[128]{0:T(128)} %copy-done.14) | copy-start | bytes 1540
Sparse Core Ops, SparseCore 0:
  11.0 105.0 all-reduce.2
  1304.8 100.6 all-reduce.4
where the time goes:
time: 1430 us; the launch traced here: 1420 us
  matrix products  482 us (34%)
  local copies, waits for them, and re-layouts  368 us (26%)
  waiting for transfers between devices  313 us (22%)
  loops' own time  128 us (9%)
  other arithmetic  99.7 us (7%)
    dot_general x76, matrix products, contract(): return jnp.einsum(pattern, operand, matrix, precision=lax.Precision.HIGHEST)  482 us
    another operation x1, loops' own time, per_device(): mixed = lax.map(mix_row, jnp.arange(grid_part, dtype=jnp.int32))  128 us
    psum x1, waiting for transfers between devices, per_device(): return lax.psum(partial_potential, 'band')  101 us
    psum x1, waiting for transfers between devices, per_device(): density = lax.psum(partial_density[0], 'band')  98.9 us
    unnamed x39, local copies, waits for them, and re-layouts  92 us
    all_to_all x1, waiting for transfers between devices, per_device(): lax.all_to_all(jnp.stack([ywave_real, ywave_imag]), 'grid', split_axis=4,...  59.3 us
    all_to_all x1, waiting for transfers between devices, per_device(): lax.all_to_all(jnp.stack([inverse_real, inverse_imag], axis=1), 'grid', s...  53 us
    all_to_all x3, local copies, waits for them, and re-layouts, per_device(): lax.all_to_all(jnp.stack([ywave_real, ywave_imag]), 'grid', split_axis=4,...  42.8 us
  transfers between devices with their start and end apart: 4, of which 4 were waited for; matrix products, arithmetic and copies ran while one was open for 1% of the time, Pallas kernels for 0%

commit v1 on v0

--- a/solution.py
+++ b/solution.py
@@ -5,6 +5,14 @@
 from jax.sharding import PartitionSpec as P
 
 N = 128
+
+
+def add_in_pairs(x, mesh_axis):
+    size, total = (lax.axis_size(mesh_axis), x)
+    for hop in [1 << k for k in range(size.bit_length() - 1)]:
+        swap = [(i, i ^ hop) for i in range(size)]
+        total = total + lax.ppermute(total, mesh_axis, swap)
+    return total
 
 
 def frequency_of(positions, length):
@@ -76,7 +84,7 @@
     first_band = band_at == 0
     lower_rows = (full_range >= 1) & (full_range < half)
     upper_rows = full_range > half
-    density = lax.psum(partial_density[0], "band")
+    density = add_in_pairs(partial_density[0], "band")
     theta_fields = density[None] * node_fields(count_nodes, node_index, node_weight)
     cosine_z, sine_z = forward_tables(full_range, own_planes, length)
     forward_real = contract("axyz,zk->axyk", theta_fields, cosine_z)

time: 1430 us -> 1500 us (1.049)
  waiting for transfers between devices: 313 us -> 385 us
    ppermute x0 -> x3, waiting for transfers between devices: none -> 170 us  [add_in_pairs(): total = total + lax.ppermute(total, mesh_axis, swap)]
    psum x1 -> x0, waiting for transfers between devices: 98.9 us -> none  [per_device(): density = lax.psum(partial_density[0], 'band')]
    unnamed x39 -> x37, local copies, waits for them, and re-layouts: 92 us -> 91 us
  transfers between devices with their start and end apart: 4 -> 6, of which waited for: 4 -> 6; matrix products, arithmetic and copies ran while one was open for 1% -> 1% of each run, Pallas kernels for 0% -> 0%
where the time goes in v1:
time: 1500 us; the launch traced here: 1490 us
  matrix products  474 us (32%)
  waiting for transfers between devices  385 us (26%)
  local copies, waits for them, and re-layouts  370 us (25%)
  loops' own time  128 us (9%)
  other arithmetic  105 us (7%)
  starting transfers between devices  17.6 us (1%)
    dot_general x76, matrix products, contract(): return jnp.einsum(pattern, operand, matrix, precision=lax.Precision.HIGHEST)  474 us
    ppermute x3, waiting for transfers between devices, add_in_pairs(): total = total + lax.ppermute(total, mesh_axis, swap)  170 us
    another operation x1, loops' own time, per_device(): mixed = lax.map(mix_row, jnp.arange(grid_part, dtype=jnp.int32))  128 us
    psum x1, waiting for transfers between devices, per_device(): return lax.psum(partial_potential, 'band')  102 us
    unnamed x37, local copies, waits for them, and re-layouts  91 us
    all_to_all x1, waiting for transfers between devices, per_device(): lax.all_to_all(jnp.stack([ywave_real, ywave_imag]), 'grid', split_axis=4,...  59.3 us
    all_to_all x1, waiting for transfers between devices, per_device(): lax.all_to_all(jnp.stack([inverse_real, inverse_imag], axis=1), 'grid', s...  53 us
    all_to_all x3, local copies, waits for them, and re-layouts, per_device(): lax.all_to_all(jnp.stack([ywave_real, ywave_imag]), 'grid', split_axis=4,...  42.8 us
  transfers between devices with their start and end apart: 6, of which 6 were waited for; matrix products, arithmetic and copies ran while one was open for 1% of the time, Pallas kernels for 0%

profile of v1, /device:TPU:0, one launch (start us, length us, event | category | flops | bytes accessed | tf_op | source)
XLA Modules:
  0.0 1493.7 jit_solution(5604005393075104709)
XLA Ops:
  9.5 45.8 %collective-permute-done = f32[32,128,128]{2,1,0:T(8,128)S(1)} collective-permute-done((f32[32,128,128]{2,1,0:T(8,128)}, f32[32,128,128]{2,1,0:T(8,128)S(1)}, u32[]{:S(2)}, u32[]{:S(2)}) %collective-permute-start) | collective-permute-done | bytes 2097184 | tf_op jit(solution)/shard_map/ppermute | solution.py:14
  59.1 45.0 %collective-permute-done.1 = f32[32,128,128]{2,1,0:T(8,128)S(1)} collective-permute-done((f32[32,128,128]{2,1,0:T(8,128)S(1)}, f32[32,128,128]{2,1,0:T(8,128)S(1)}, u32[]{:S(2)}, u32[]{:S(2)}) %collective-permute-start.1) | collective-permute-done | bytes 2097184 | tf_op jit(solution)/shard_map/ppermute | solution.py:14
  118.3 79.5 %collective-permute-done.2 = f32[32,128,128]{2,1,0:T(8,128)} collective-permute-done((f32[32,128,128]{2,1,0:T(8,128)}, f32[32,128,128]{2,1,0:T(8,128)}, u32[]{:S(2)}, u32[]{:S(2)}) %collective-permute-start.2) | collective-permute-done | bytes 2097184 | tf_op jit(solution)/shard_map/ppermute | solution.py:14
  201.7 57.8 %fusion.70 = f32[1,20,32,128,8]{3,4,2,1,0:T(8,128)} fusion(f32[32,128,128]{2,1,0:T(8,128)} %get-tuple-element.295, s32[32,128,128]{2,1,0:T(8,128)} %get-tuple-element.309, f32[32,128,128]{2,1,0:T(8,128)} %get-tuple-element.296, s32[32,128,128]{2,1,0:T(8,128)} %get-tuple-element.310, f32[32,128,128]{2,1,0:T(8,128)} %get-tuple-element.294, ...), kind=kOutput, calls=%fused_computation.132 | convolution fusion | flops 1132476416 | bytes 21495840 | tf_op jit(solution)/shard_map/axyz,zk->axyk/dot_general | solution.py:47
  259.5 57.5 %negate_bitcast_fusion = f32[1,20,32,128,8]{3,4,2,1,0:T(8,128)} fusion(f32[32,128,128]{2,1,0:T(8,128)} %get-tuple-element.295, s32[32,128,128]{2,1,0:T(8,128)} %get-tuple-element.309, f32[32,128,128]{2,1,0:T(8,128)} %get-tuple-element.296, s32[32,128,128]{2,1,0:T(8,128)} %get-tuple-element.310, f32[32,128,128]{2,1,0:T(8,128)} %get-tuple-element.294, ...), kind=kOutput, calls=%fused_computation.123 | convolution fusion | flops 1133132800 | bytes 21496360 | tf_op jit(solution)/shard_map/axyz,zk->axyk/dot_general | solution.py:47
  351.0 9.3 scatter.14
  364.8 17.6 %copy.61 = f32[2,20,32,8,128]{2,3,1,0,4:T(8,128)} copy(f32[2,20,32,8,128]{4,3,2,1,0:T(8,128)} %pad_maximum_fusion.1) | data formatting | bytes 10485760 | tf_op jit(solution)/shard_map/stack | solution.py:115
  382.5 23.5 %reshape.667 = f32[4,1,327680]{2,1,0:T(1,128)} reshape(f32[128,2,20,8,32]{4,3,2,1,0:T(8,128)} %bitcast.307) | data formatting | bytes 10485760
  411.2 59.3 %all-to-all-done = f32[4,1,327680]{2,1,0:T(1,128)} async-done(((f32[4,1,327680]{2,1,0:T(1,128)}), f32[4,1,327680]{2,1,0:T(1,128)}, u32[]{:S(2)}, u32[]{:S(2)}) %all-to-all-start) | async-done | bytes 5242912 | tf_op jit(solution)/shard_map/all_to_all | solution.py:114
  471.0 17.8 %reduce.21 = f32[4,327680]{1,0:T(4,128)} reduce(f32[4,1,327680]{2,1,0:T(1,128)} %all-to-all-done, f32[]{:T(128)} %broadcast.766), dimensions={1}, to_apply=%all_to_all.26.reduce_sub_computation | reduce | bytes 10485764 | tf_op jit(solution)/shard_map/all_to_all | solution.py:114
  488.9 16.7 %reshape.668 = f32[128,2,20,8,32]{4,3,2,1,0:T(8,128)} reshape(f32[4,327680]{1,0:T(4,128)} %reduce.21) | data formatting | bytes 10485760
  505.6 25.8 %copy.142 = f32[2,20,32,8,4,32]{2,4,5,3,1,0:T(4,128)} copy(f32[2,20,32,8,4,32]{2,3,1,0,5,4:T(8,128)} %bitcast.308) | data formatting | bytes 10485760 | tf_op jit(solution)/shard_map/all_to_all | solution.py:114
  531.4 16.5 %all_to_all.29 = f32[2,20,128,8,32]{2,4,3,1,0:T(8,128)} reshape(f32[2,20,4,32,8,32]{3,2,5,4,1,0:T(4,128)} %bitcast.309) | data formatting | bytes 10485760 | tf_op jit(solution)/shard_map/all_to_all | solution.py:114
  564.2 424.3 %while.20 = (s32[]{:T(128)}, f32[32,2,20,8,128]{4,3,2,1,0:T(8,128)}, s32[32]{0:T(128)S(1)}, f32[20,8,32,128]{3,2,1,0:T(8,128)}, s32[8,32]{0,1:T(8,128)S(1)}, /*i...) while((s32[]{:T(128)}, ...), condition=%wide.region_1.2_spmd.clone.clone, body=%wide.region_0.1_spmd.clone.clone.sunk | while | flops 633025536 | bytes 4581378 | solution.py:155
  1004.0 17.6 %copy.63 = f32[32,2,20,8,128]{0,3,2,1,4:T(8,128)} copy(f32[32,2,20,8,128]{4,3,2,1,0:T(8,128)} %pad_maximum_fusion.2) | data formatting | bytes 10485760 | tf_op jit(solution)/shard_map/stack | solution.py:161
  1021.6 23.5 %reshape.669 = f32[4,1,327680]{2,1,0:T(1,128)} reshape(f32[128,2,20,8,32]{4,3,2,1,0:T(8,128)} %bitcast.310) | data formatting | bytes 10485760
  1056.6 53.0 %all-to-all-done.1 = f32[4,1,327680]{2,1,0:T(1,128)} async-done(((f32[4,1,327680]{2,1,0:T(1,128)}), f32[4,1,327680]{2,1,0:T(1,128)}, u32[]{:S(2)}, u32[]{:S(2)}) %all-to-all-start.1) | async-done | bytes 5242912 | tf_op jit(solution)/shard_map/all_to_all | solution.py:160
  1109.6 18.2 %reduce.22 = f32[4,327680]{1,0:T(4,128)} reduce(f32[4,1,327680]{2,1,0:T(1,128)} %all-to-all-done.1, f32[]{:T(128)} %broadcast.766), dimensions={1}, to_apply=%all_to_all.30.reduce_sub_computation | reduce | bytes 10485764 | tf_op jit(solution)/shard_map/all_to_all | solution.py:160
  1127.8 16.7 %reshape.670 = f32[128,2,20,8,32]{4,3,2,1,0:T(8,128)} reshape(f32[4,327680]{1,0:T(4,128)} %reduce.22) | data formatting | bytes 10485760
  1144.5 25.5 %copy.64 = f32[4,32,2,20,8,32]{1,0,5,3,4,2:T(4,128)} copy(f32[4,32,2,20,8,32]{1,4,3,2,5,0:T(8,128)} %bitcast.311) | data formatting | bytes 10485760 | tf_op jit(solution)/shard_map/all_to_all | solution.py:160
  1170.1 16.7 %all_to_all.33 = f32[128,2,20,8,32]{0,4,2,3,1:T(8,128)} reshape(f32[4,32,2,20,8,32]{1,0,5,3,4,2:T(4,128)} %copy.64) | data formatting | bytes 10485760 | tf_op jit(solution)/shard_map/all_to_all | solution.py:160
  1215.4 69.8 %fusion.68 = f32[20,32,128,128]{3,2,1,0:T(8,128)} fusion(f32[20,8,32,128]{3,2,1,0:T(8,128)S(1)} %get-tuple-element.284, s32[8]{0:T(128)S(1)} %iota_add_fusion.1, pred[8]{0:T(512)(128)(4,1)S(1)} %broadcast_compare_fusion), kind=kOutput, calls=%fused_computation.121 | convolution fusion | flops 1006649344 | bytes 44564520 | tf_op jit(solution)/shard_map/bpxy,pz->bxyz/dot_general | solution.py:47
  1285.3 95.9 %multiply_reduce_fusion.4 = f32[32,128,128]{2,1,0:T(8,128)} fusion(f32[20,32,128,128]{3,2,1,0:T(8,128)} %fusion.68, f32[32,128,128]{2,1,0:T(8,128)S(1)} %copy-done.6, f32[32,128,128]{2,1,0:T(8,128)S(1)} %copy-done.7, f32[32,128,128]{2,1,0:T(8,128)S(1)} %copy-done.5, f32[32,128,128]{2,1,0:T(8,128)S(1)} %get-tuple-element.289, ...), kind=kOutput, calls=%fused_computation.74 | convolution fusion | flops 1163411456 | bytes 63439400 | tf_op jit(solution)/shard_map/bpxy,pz->bxyz/dot_general | solution.py:47
  1381.2 102.3 %all-reduce.2.cloned.1.call-done = f32[32,128,128]{2,1,0:T(8,128)} async-done(((f32[32,128,128]{2,1,0:T(8,128)}), f32[32,128,128]{2,1,0:T(8,128)}) %all-reduce.2.cloned.1.call-update) | async-done | bytes 2097168 | tf_op jit(solution)/shard_map/psum | solution.py:196
  (1145 shorter events, 440.2 us)
Async XLA Ops:
  6.5 101.8 %copy-start = (s32[32,128,128]{2,1,0:T(8,128)S(1)}, s32[32,128,128]{2,1,0:T(8,128)}, u32[]{:S(2)}) copy-start(s32[32,128,128]{2,1,0:T(8,128)} %param.20) | copy-start | bytes 6291460
  6.5 48.8 %collective-permute-start = (f32[32,128,128]{2,1,0:T(8,128)}, f32[32,128,128]{2,1,0:T(8,128)S(1)}, u32[]{:S(2)}, u32[]{:S(2)}) collective-permute-start(f32[32,128,128]{2,1,0:T(8,128)} %bitcast.330), channel_id=1, source_target_pairs={{0,4},{4,0},{8,12},{12,8},{16,20},{20,16},{24,28},{28,24},{1,5},{5... | collective-permute-start | bytes 6291464 | tf_op jit(solution)/shard_map/ppermute | solution.py:14
  57.2 46.9 %collective-permute-start.1 = (f32[32,128,128]{2,1,0:T(8,128)S(1)}, f32[32,128,128]{2,1,0:T(8,128)S(1)}, u32[]{:S(2)}, u32[]{:S(2)}) collective-permute-start(f32[32,128,128]{2,1,0:T(8,128)S(1)} %bitcast_add_fusion.1), channel_id=1, source_target_pairs={{0,8},{4,12},{8,0},{12,4},{16,24},{20,28},{24,16},{28,20},{1,9},{5... | collective-permute-start | bytes 6291464 | tf_op jit(solution)/shard_map/ppermute | solution.py:14
  105.7 92.1 %collective-permute-start.2 = (f32[32,128,128]{2,1,0:T(8,128)}, f32[32,128,128]{2,1,0:T(8,128)}, u32[]{:S(2)}, u32[]{:S(2)}) collective-permute-start(f32[32,128,128]{2,1,0:T(8,128)} %add.498), channel_id=1, source_target_pairs={{0,16},{4,20},{8,24},{12,28},{16,0},{20,4},{24,8},{28,12},{1,17},{... | collective-permute-start | bytes 6291464 | tf_op jit(solution)/shard_map/ppermute | solution.py:14
  108.3 151.3 %copy-start.13 = (f32[128]{0:T(128)}, f32[128]{0:T(128)S(1)}, u32[]{:S(2)}) copy-start(f32[128]{0:T(128)S(1)} %fusion.141) | copy-start | bytes 1540
  317.1 7.3 copy-start.10
  317.1 7.3 copy-start.11
  406.0 64.5 %all-to-all-start = ((f32[4,1,327680]{2,1,0:T(1,128)}), f32[4,1,327680]{2,1,0:T(1,128)}, u32[]{:S(2)}, u32[]{:S(2)}) async-start(f32[4,1,327680]{2,1,0:T(1,128)} %reshape.667), calls=%async_computation | async-start | bytes 10485760 | tf_op jit(solution)/shard_map/all_to_all | solution.py:114
  547.9 8.8 copy-start.8
  561.1 3.1 copy-start.12
  988.5 7.3 copy-start.9
  1045.1 64.5 %all-to-all-start.1 = ((f32[4,1,327680]{2,1,0:T(1,128)}), f32[4,1,327680]{2,1,0:T(1,128)}, u32[]{:S(2)}, u32[]{:S(2)}) async-start(f32[4,1,327680]{2,1,0:T(1,128)} %reshape.669), calls=%async_computation.1 | async-start | bytes 10485760 | tf_op jit(solution)/shard_map/all_to_all | solution.py:160
  1050.1 433.4 %all-reduce.2.cloned.1.call-start = ((), (), s32[]{:S(2)}) async-start(), calls=%async_computation.2 | async-start | bytes 4194304 | tf_op jit(solution)/shard_map/psum | solution.py:196
  1215.3 69.9 %copy-start.1 = (s32[32,128,128]{2,1,0:T(8,128)S(1)}, s32[32,128,128]{2,1,0:T(8,128)}, u32[]{:S(2)}) copy-start(s32[32,128,128]{2,1,0:T(8,128)} %param.20) | copy-start | bytes 6291460
  1215.3 69.9 %copy-start.2 = (s32[32,128,128]{2,1,0:T(8,128)S(1)}, s32[32,128,128]{2,1,0:T(8,128)}, u32[]{:S(2)}) copy-start(s32[32,128,128]{2,1,0:T(8,128)} %get-tuple-element.308) | copy-start | bytes 6291460
  1215.4 69.9 %copy-start.3 = (s32[32,128,128]{2,1,0:T(8,128)S(1)}, s32[32,128,128]{2,1,0:T(8,128)}, u32[]{:S(2)}) copy-start(s32[32,128,128]{2,1,0:T(8,128)} %get-tuple-element.309) | copy-start | bytes 6291460
  1215.4 69.9 %copy-start.4 = (s32[32,128,128]{2,1,0:T(8,128)S(1)}, s32[32,128,128]{2,1,0:T(8,128)}, u32[]{:S(2)}) copy-start(s32[32,128,128]{2,1,0:T(8,128)} %get-tuple-element.310) | copy-start | bytes 6291460
  1215.4 69.9 %copy-start.5 = (f32[32,128,128]{2,1,0:T(8,128)S(1)}, f32[32,128,128]{2,1,0:T(8,128)}, u32[]{:S(2)}) copy-start(f32[32,128,128]{2,1,0:T(8,128)} %get-tuple-element.290) | copy-start | bytes 6291460
  1215.4 69.9 %copy-start.6 = (f32[32,128,128]{2,1,0:T(8,128)S(1)}, f32[32,128,128]{2,1,0:T(8,128)}, u32[]{:S(2)}) copy-start(f32[32,128,128]{2,1,0:T(8,128)} %get-tuple-element.291) | copy-start | bytes 6291460
  1215.4 69.9 %copy-start.7 = (f32[32,128,128]{2,1,0:T(8,128)S(1)}, f32[32,128,128]{2,1,0:T(8,128)}, u32[]{:S(2)}) copy-start(f32[32,128,128]{2,1,0:T(8,128)} %get-tuple-element.292) | copy-start | bytes 6291460
  1215.4 69.9 %copy-start.14 = (f32[128]{0:T(128)S(1)}, f32[128]{0:T(128)}, u32[]{:S(2)}) copy-start(f32[128]{0:T(128)} %copy-done.13) | copy-start | bytes 1540
Sparse Core Ops, SparseCore 0:
  1381.4 102.1 all-reduce.1
